TPU v7x, 32 devices: a whole 2x2x4 slice. The times are simulated.
32 devices in a mesh: groups: 1, row: 4 (over z), col: 4 (over y, x), ksplit: 2 (over core).
Axes of the slice: x: 2, y: 2, z: 4, core: 2. Of those that a mesh axis runs over, the one named last changes fastest.
Arguments:
- pair_state: bfloat16 [128, 128, 128], P(('groups', 'row'), ('col', 'ksplit')), may hold values from -6 to 6
- residue_mask: int32 [128], P('groups'), may hold values 0 or 1
- input_gain: float32 [128], replicated, may hold values from 0.1 to 1.9
- input_shift: float32 [128], replicated, may hold values from -3 to 3
- left_right: bfloat16 [128, 512], replicated, may hold values from -0.5 to 0.5
- output_gate: bfloat16 [128, 128], replicated, may hold values from -0.5 to 0.5
- final_gain: float32 [128], replicated, may hold values from 0.1 to 1.9
- final_shift: float32 [128], replicated, may hold values from -3 to 3
- output_weight: bfloat16 [128, 128], replicated, may hold values from -0.5 to 0.5
Outputs:
- pair_update: bfloat16 [128, 128, 128], P(('groups', 'row'), ('col', 'ksplit'))
All inputs are finite; a program needn't handle non-finite values.
Results may differ from a plain program's by a relative error of at most 0.0053.
Values may be sent and summed in bfloat16 or wider, within the bound.
A program may use at most 64 MiB of HBM per device.

v0:
```python
import jax
import jax.numpy as jnp
from jax import lax
from jax.sharding import PartitionSpec as P


def norm_over(data, norm_gain, norm_shift, over_axis):
    average = jnp.mean(data, axis=over_axis, keepdims=True)
    centred = data - average
    spread = jnp.mean(centred * centred, axis=over_axis, keepdims=True)
    return centred * lax.rsqrt(spread + 1e-05) * norm_gain + norm_shift


def gated_side(normed_in, weights, live_mask, hidden):
    values = jnp.einsum(
        "ikc,ch->hik", normed_in, weights[:, :hidden], preferred_element_type=jnp.float32
    )
    gates = jnp.einsum(
        "ikc,ch->hik", normed_in, weights[:, hidden:], preferred_element_type=jnp.float32
    )
    return (live_mask * jax.nn.sigmoid(gates) * values).astype(jnp.bfloat16)


def contract_parts(left_parts, right_parts, row_count, col_count):
    count_items = left_parts.shape[2]
    tile_rows = left_parts.shape[3]
    tile_cols = left_parts.shape[4]

    def assemble(parts):
        return parts.transpose(2, 0, 3, 1, 4).reshape(
            count_items, row_count * tile_rows, col_count * tile_cols
        )

    products = jnp.einsum(
        "cik,cjk->cij",
        assemble(left_parts),
        assemble(right_parts),
        preferred_element_type=jnp.float32,
    )
    returned = products.reshape(count_items, row_count, tile_rows, col_count, tile_cols)
    return returned.transpose(1, 3, 0, 2, 4)


def body(
    pair_state,
    residue_mask,
    input_gain,
    input_shift,
    left_right,
    output_gate,
    final_gain,
    final_shift,
    output_weight,
):
    tile_rows, tile_cols, channels = pair_state.shape
    hidden = output_weight.shape[0]
    normed_in = norm_over(pair_state.astype(jnp.float32), input_gain, input_shift, 2).astype(
        jnp.bfloat16
    )
    row_start = lax.axis_index("row") * tile_rows
    col_start = lax.axis_index(("col", "ksplit")) * tile_cols
    row_live = lax.dynamic_slice_in_dim(residue_mask, row_start, tile_rows).astype(jnp.float32)
    col_live = lax.dynamic_slice_in_dim(residue_mask, col_start, tile_cols).astype(jnp.float32)
    live_mask = row_live[:, None] * col_live[None, :]
    left_side = gated_side(normed_in, left_right[:, : 2 * hidden], live_mask, hidden)
    right_side = gated_side(normed_in, left_right[:, 2 * hidden :], live_mask, hidden)
    devices_all = lax.axis_size(("row", "col", "ksplit"))
    row_count = lax.axis_size("row")
    col_count = devices_all // row_count
    per_device = hidden // devices_all
    grouped_left = left_side.reshape(devices_all, per_device, tile_rows, tile_cols)
    grouped_right = right_side.reshape(devices_all, per_device, tile_rows, tile_cols)
    left_parts = lax.all_to_all(
        grouped_left, ("row", "col", "ksplit"), split_axis=0, concat_axis=0, tiled=True
    )
    right_parts = lax.all_to_all(
        grouped_right, ("row", "col", "ksplit"), split_axis=0, concat_axis=0, tiled=True
    )
    count_items = left_parts.shape[1]
    shaped_left = left_parts.reshape(row_count, col_count, count_items, tile_rows, tile_cols)
    shaped_right = right_parts.reshape(row_count, col_count, count_items, tile_rows, tile_cols)
    returned = contract_parts(shaped_left, shaped_right, row_count, col_count)
    returned = returned.reshape(devices_all, count_items, tile_rows, tile_cols)
    received = lax.all_to_all(
        returned, ("row", "col", "ksplit"), split_axis=0, concat_axis=0, tiled=True
    )
    mixed_tile = received.reshape(hidden, tile_rows, tile_cols)
    normed_out = norm_over(
        mixed_tile, final_gain[:, None, None], final_shift[:, None, None], 0
    ).astype(jnp.bfloat16)
    projected_out = jnp.einsum(
        "hij,hc->ijc", normed_out, output_weight, preferred_element_type=jnp.float32
    )
    gate_values = jax.nn.sigmoid(
        jnp.einsum("ijc,cd->ijd", normed_in, output_gate, preferred_element_type=jnp.float32)
    )
    return (gate_values * projected_out).astype(jnp.bfloat16)


def solution(mesh):
    placed = (
        P(("groups", "row"), ("col", "ksplit"), None),
        P("groups"),
        P(),
        P(),
        P(),
        P(),
        P(),
        P(),
        P(),
    )
    return jax.shard_map(
        body,
        mesh=mesh,
        in_specs=placed,
        out_specs=P(("groups", "row"), ("col", "ksplit"), None),
        check_vma=False,
    )
```

profile of v0, /device:TPU:0, one launch (start us, length us, event | category | flops | bytes accessed | tf_op | source)
XLA Modules:
  0.0 53.6 jit_solution(15498445328128117906)
XLA Ops:
  0.0 0.8 %dynamic-slice_convert_fusion = f32[16]{0:T(128)S(1)} fusion(s32[128]{0:T(128)} %param.10, s32[]{:T(128)S(6)} %select_n.7), kind=kLoop, calls=%fused_computation.53 | loop fusion | flops 16 | bytes 132 | tf_op jit(solution)/shard_map/convert_element_type | solution.py:63
  0.8 0.7 %dynamic-slice_convert_fusion.1 = f32[32]{0:T(128)S(1)} fusion(s32[128]{0:T(128)} %param.10, s32[]{:T(128)S(6)} %select_n.6), kind=kLoop, calls=%fused_computation.54 | loop fusion | flops 32 | bytes 260 | tf_op jit(solution)/shard_map/convert_element_type | solution.py:62
  1.5 1.0 %convert_reduce_fusion = f32[32,16]{1,0:T(8,128)S(1)} fusion(bf16[32,16,128]{2,1,0:T(8,128)(2,1)} %param.9), kind=kLoop, calls=%fused_computation.31 | loop fusion | flops 130560 | bytes 133120 | tf_op jit(solution)/shard_map/reduce_sum | solution.py:8
  2.5 0.1 copy.49
  2.6 0.1 copy.50
  2.7 0.2 fusion.22
  3.0 0.1 copy.51
  3.0 0.1 copy.52
  3.1 0.1 broadcast_multiply_fusion
  3.2 0.3 copy-done.2
  3.5 0.3 copy-done.4
  3.8 0.0 copy-done.5
  3.8 0.3 fusion.7
  4.2 0.3 fusion.15
  4.5 0.5 copy.53
  5.0 1.2 %reshape.97 = bf16[32,2,1024]{2,1,0:T(2,128)(2,1)} reshape(bf16[32,4,16,32]{3,2,1,0:T(8,128)(2,1)S(1)} %bitcast.64) | data formatting | bytes 262144
  6.1 7.3 %all-to-all-start = ((bf16[32,2,1024]{2,1,0:T(2,128)(2,1)}), bf16[32,2,1024]{2,1,0:T(2,128)(2,1)S(1)}, u32[]{:S(2)}, u32[]{:S(2)}) async-start(bf16[32,2,1024]{2,1,0:T(2,128)(2,1)} %reshape.97), calls=%async_computation | async-start | bytes 262144 | tf_op jit(solution)/shard_map/all_to_all | solution.py:73
  13.5 0.3 fusion.3
  13.8 0.3 fusion.14
  14.1 0.5 copy.55
  14.6 1.2 %reshape.99 = bf16[32,2,1024]{2,1,0:T(2,128)(2,1)} reshape(bf16[32,4,16,32]{3,2,1,0:T(8,128)(2,1)S(1)} %bitcast.65) | data formatting | bytes 262144
  15.8 5.9 %all-to-all-done = bf16[32,2,1024]{2,1,0:T(2,128)(2,1)S(1)} async-done(((bf16[32,2,1024]{2,1,0:T(2,128)(2,1)}), bf16[32,2,1024]{2,1,0:T(2,128)(2,1)S(1)}, u32[]{:S(2)}, u32[]{:S(2)}) %all-to-all-start) | async-done | bytes 131104 | tf_op jit(solution)/shard_map/all_to_all | solution.py:73
  21.7 2.6 %all-to-all-start.1 = ((bf16[32,2,1024]{2,1,0:T(2,128)(2,1)}), bf16[32,2,1024]{2,1,0:T(2,128)(2,1)S(1)}, u32[]{:S(2)}, u32[]{:S(2)}) async-start(bf16[32,2,1024]{2,1,0:T(2,128)(2,1)} %reshape.99), calls=%async_computation.1 | async-start | bytes 262144 | tf_op jit(solution)/shard_map/all_to_all | solution.py:76
  24.3 0.3 reshape.98
  24.5 0.4 copy.68
  24.9 0.3 reshape.84
  25.2 7.2 %all-to-all-done.1 = bf16[32,2,1024]{2,1,0:T(2,128)(2,1)S(1)} async-done(((bf16[32,2,1024]{2,1,0:T(2,128)(2,1)}), bf16[32,2,1024]{2,1,0:T(2,128)(2,1)S(1)}, u32[]{:S(2)}, u32[]{:S(2)}) %all-to-all-start.1) | async-done | bytes 131104 | tf_op jit(solution)/shard_map/all_to_all | solution.py:76
  32.5 0.3 reshape.100
  32.7 0.4 copy.67
  33.1 0.3 reshape.87
  33.4 0.2 fusion.41
  33.7 0.4 reshape.88
  34.1 0.1 copy.60
  34.2 1.2 %reshape.101 = f32[32,1,2048]{2,1,0:T(1,128)} reshape(f32[32,4,16,32]{3,2,1,0:T(8,128)S(1)} %bitcast.63) | data formatting | bytes 524288
  35.4 2.6 %all-to-all-start.2 = ((f32[32,1,2048]{2,1,0:T(1,128)}), f32[32,1,2048]{2,1,0:T(1,128)S(1)}, u32[]{:S(2)}, u32[]{:S(2)}) async-start(f32[32,1,2048]{2,1,0:T(1,128)} %reshape.101), calls=%async_computation.2 | async-start | bytes 524288 | tf_op jit(solution)/shard_map/all_to_all | solution.py:84
  38.0 0.3 fusion.10
  38.3 10.2 %all-to-all-done.2 = f32[32,1,2048]{2,1,0:T(1,128)S(1)} async-done(((f32[32,1,2048]{2,1,0:T(1,128)}), f32[32,1,2048]{2,1,0:T(1,128)S(1)}, u32[]{:S(2)}, u32[]{:S(2)}) %all-to-all-start.2) | async-done | bytes 262176 | tf_op jit(solution)/shard_map/all_to_all | solution.py:84
  48.6 0.5 broadcast.85
  49.1 1.3 %reduce.2 = f32[32,2048]{1,0:T(8,128)S(1)} reduce(f32[32,1,2048]{2,1,0:T(1,128)S(1)} %all-to-all-done.2, f32[]{:T(128)} %broadcast.85), dimensions={1}, to_apply=%all_to_all.11.reduce_sub_computation | reduce | bytes 524292 | tf_op jit(solution)/shard_map/all_to_all | solution.py:84
  50.3 0.3 reshape.102
  50.7 0.1 bitcast_reduce_fusion
  50.8 0.2 multiply_reduce_fusion
  51.1 0.6 %copy-done.6 = f32[128]{0:T(128)S(1)} copy-done((f32[128]{0:T(128)S(1)}, f32[128]{0:T(128)}, u32[]{:S(2)}) %copy-start.6) | copy-done | bytes 536
  51.7 0.0 copy-done.7
  51.7 0.3 fusion.19
  52.1 0.5 copy.61
  52.6 0.2 copy-done.3
  52.8 0.8 %fusion.13 = bf16[32,16,128]{2,1,0:T(8,128)(2,1)} fusion(f32[32,16,128]{2,1,0:T(8,128)S(1)} %fusion.10, bf16[128,32,16]{0,2,1:T(8,128)(2,1)S(1)} %copy.61, bf16[128,128]{1,0:T(8,128)(2,1)S(1)} %copy-done.3), kind=kOutput, calls=%fused_computation.19 | convolution fusion | flops 16908288 | bytes 557056 | tf_op jit(solution)/shard_map/hij,hc->ijc/dot_general | solution.py:91
  (14 shorter events, 0.1 us)
Async XLA Ops:
  0.0 38.0 %copy-start = (bf16[128,128]{1,0:T(8,128)(2,1)S(1)}, bf16[128,128]{1,0:T(8,128)(2,1)}, u32[]{:S(2)}) copy-start(bf16[128,128]{1,0:T(8,128)(2,1)} %param.14) | copy-start | bytes 98308
  0.0 2.7 %copy-start.1 = (bf16[32,16,128]{2,1,0:T(8,128)(2,1)S(1)}, bf16[32,16,128]{2,1,0:T(8,128)(2,1)}, u32[]{:S(2)}) copy-start(bf16[32,16,128]{2,1,0:T(8,128)(2,1)} %param.9) | copy-start | bytes 393220
  2.6 0.9 %copy-start.2 = (bf16[128,512]{1,0:T(8,128)(2,1)S(1)}, bf16[128,512]{1,0:T(8,128)(2,1)}, u32[]{:S(2)}) copy-start(bf16[128,512]{1,0:T(8,128)(2,1)} %param.13) | copy-start | bytes 393220
  3.1 0.7 %copy-start.4 = (f32[128]{0:T(128)S(1)}, f32[128]{0:T(128)}, u32[]{:S(2)}) copy-start(f32[128]{0:T(128)} %param.12) | copy-start | bytes 1540
  3.1 0.7 %copy-start.5 = (f32[128]{0:T(128)S(1)}, f32[128]{0:T(128)}, u32[]{:S(2)}) copy-start(f32[128]{0:T(128)} %param.11) | copy-start | bytes 1540
  6.1 15.5 %all-to-all-start = ((bf16[32,2,1024]{2,1,0:T(2,128)(2,1)}), bf16[32,2,1024]{2,1,0:T(2,128)(2,1)S(1)}, u32[]{:S(2)}, u32[]{:S(2)}) async-start(bf16[32,2,1024]{2,1,0:T(2,128)(2,1)} %reshape.97), calls=%async_computation | async-start | bytes 262144 | tf_op jit(solution)/shard_map/all_to_all | solution.py:73
  21.7 10.8 %all-to-all-start.1 = ((bf16[32,2,1024]{2,1,0:T(2,128)(2,1)}), bf16[32,2,1024]{2,1,0:T(2,128)(2,1)S(1)}, u32[]{:S(2)}, u32[]{:S(2)}) async-start(bf16[32,2,1024]{2,1,0:T(2,128)(2,1)} %reshape.99), calls=%async_computation.1 | async-start | bytes 262144 | tf_op jit(solution)/shard_map/all_to_all | solution.py:76
  35.4 13.2 %all-to-all-start.2 = ((f32[32,1,2048]{2,1,0:T(1,128)}), f32[32,1,2048]{2,1,0:T(1,128)S(1)}, u32[]{:S(2)}, u32[]{:S(2)}) async-start(f32[32,1,2048]{2,1,0:T(1,128)} %reshape.101), calls=%async_computation.2 | async-start | bytes 524288 | tf_op jit(solution)/shard_map/all_to_all | solution.py:84
  51.0 0.7 %copy-start.6 = (f32[128]{0:T(128)S(1)}, f32[128]{0:T(128)}, u32[]{:S(2)}) copy-start(f32[128]{0:T(128)} %param.16) | copy-start | bytes 1540
  51.0 0.7 %copy-start.7 = (f32[128]{0:T(128)S(1)}, f32[128]{0:T(128)}, u32[]{:S(2)}) copy-start(f32[128]{0:T(128)} %param.15) | copy-start | bytes 1540
  52.1 0.8 %copy-start.3 = (bf16[128,128]{1,0:T(8,128)(2,1)S(1)}, bf16[128,128]{1,0:T(8,128)(2,1)}, u32[]{:S(2)}) copy-start(bf16[128,128]{1,0:T(8,128)(2,1)} %param.17) | copy-start | bytes 98308
where the time goes:
time: 54.1 us; the launch traced here: 53.6 us
  waiting for transfers between devices  23.4 us (43%)
  starting transfers between devices  12.5 us (23%)
  local copies, waits for them, and re-layouts  10.1 us (19%)
  other arithmetic  4.81 us (9%)
  matrix products  2.71 us (5%)
    all_to_all x1, waiting for transfers between devices, body(): lax.all_to_all(returned, ('row', 'col', 'ksplit'), split_axis=0, concat_a...  10.2 us
    all_to_all x1, starting transfers between devices, body(): lax.all_to_all(grouped_left, ('row', 'col', 'ksplit'), split_axis=0, conc...  7.33 us
    all_to_all x1, waiting for transfers between devices, body(): lax.all_to_all(grouped_right, ('row', 'col', 'ksplit'), split_axis=0, con...  7.24 us
    all_to_all x1, waiting for transfers between devices, body(): lax.all_to_all(grouped_left, ('row', 'col', 'ksplit'), split_axis=0, conc...  5.9 us
    unnamed x22, local copies, waits for them, and re-layouts  5.88 us
    all_to_all x1, starting transfers between devices, body(): lax.all_to_all(returned, ('row', 'col', 'ksplit'), split_axis=0, concat_a...  2.58 us
    all_to_all x1, starting transfers between devices, body(): lax.all_to_all(grouped_right, ('row', 'col', 'ksplit'), split_axis=0, con...  2.57 us
    all_to_all x1, other arithmetic, body(): lax.all_to_all(returned, ('row', 'col', 'ksplit'), split_axis=0, concat_a...  1.26 us
  transfers between devices with their start and end apart: 3, of which 3 were waited for; matrix products, arithmetic and copies ran while one was open for 7% of the time, Pallas kernels for 0%

commit v1 on v0

--- a/solution.py
+++ b/solution.py
@@ -1,7 +1,316 @@
+import functools
+
 import jax
 import jax.numpy as jnp
 from jax import lax
+from jax.experimental import pallas as pl
+from jax.experimental.pallas import tpu as pltpu
 from jax.sharding import PartitionSpec as P
+
+MESH = pl.DeviceIdType.MESH
+LANES = 128
+F32 = jnp.float32
+BF16 = jnp.bfloat16
+BACK = jnp.bfloat16
+
+
+def norm_rows(data, gain, shift):
+    average = jnp.mean(data, axis=-1, keepdims=True)
+    centred = data - average
+    spread = jnp.mean(centred * centred, axis=-1, keepdims=True)
+    return centred * lax.rsqrt(spread + 1e-05) * gain + shift
+
+
+def swap_blocks(parts, width):
+    count = len(parts)
+    lane_block = lax.broadcasted_iota(jnp.int32, parts[0].shape, 1) // width
+    parts = list(parts)
+    step = count // 2
+    while step:
+        upper = (lane_block & step) != 0
+        for low in range(count):
+            if low & step:
+                continue
+            first, second = parts[low], parts[low + step]
+            parts[low] = jnp.where(upper, pltpu.roll(second, step * width, 1), first)
+            parts[low + step] = jnp.where(
+                upper, second, pltpu.roll(first, LANES - step * width, 1)
+            )
+        step //= 2
+    return parts
+
+
+def kernel(
+    sizes,
+    state_ref,
+    mask_scalars,
+    mask_ref,
+    input_gain,
+    input_shift,
+    left_right,
+    output_gate,
+    final_gain,
+    final_shift,
+    output_weight,
+    out_ref,
+    normed_buf,
+    gate_buf,
+    left_stage,
+    right_stage,
+    send,
+    recv,
+    back,
+    home,
+    send_sem,
+    recv_sem,
+    back_sem,
+    home_sem,
+):
+    row_count, col_count, split_count, tile_rows, tile_cols, channels, hidden = sizes
+    plane = col_count * split_count
+    devices = row_count * plane
+    blocks = LANES // tile_rows
+    my_row = lax.axis_index("row")
+    my_plane = lax.axis_index("col") * split_count + lax.axis_index("ksplit")
+    me = my_row * plane + my_plane
+
+    def place(index):
+        within = lax.rem(index, plane)
+        return {
+            "row": index // plane,
+            "col": within // split_count,
+            "ksplit": lax.rem(within, split_count),
+        }
+
+    barrier = pltpu.get_barrier_semaphore()
+
+    def greet(step, carry):
+        pl.semaphore_signal(
+            barrier, inc=1, device_id=place(lax.rem(me + step, devices)), device_id_type=MESH
+        )
+        return carry
+
+    lax.fori_loop(1, devices, greet, 0)
+
+    positions = tile_rows * tile_cols
+    state = state_ref[...].astype(F32).reshape(positions, channels)
+    normed = norm_rows(state, input_gain[...], input_shift[...]).astype(BF16)
+    normed_buf[...] = normed.astype(F32)
+    weights = jnp.transpose(left_right[...].astype(F32)).astype(BF16)
+
+    lane_block = lax.broadcasted_iota(jnp.int32, (tile_rows, LANES), 1) // tile_rows
+    mask_rows = jnp.broadcast_to(mask_ref[...].astype(F32), (tile_rows, LANES))
+    row_live = mask_rows
+    turn = lax.rem(lane_block - my_row + row_count, row_count)
+    for shift in range(1, blocks):
+        row_live = jnp.where(turn == shift, pltpu.roll(mask_rows, shift * tile_rows, 1), row_live)
+
+    for quarter in range(tile_cols // blocks):
+        rows = []
+        col_live = jnp.zeros((tile_rows, LANES), F32)
+        for inner in range(blocks):
+            k = quarter * blocks + inner
+            rows.append(normed_buf[pl.ds(k, tile_rows, stride=tile_cols), :])
+            alive = mask_scalars[my_plane * tile_cols + k].astype(F32)
+            col_live = jnp.where(lane_block == inner, alive, col_live)
+        live = row_live * col_live
+        packed = jnp.concatenate(rows, axis=0).astype(BF16)
+        projected = lax.dot_general(
+            weights, packed, (((1,), (1,)), ((), ())), preferred_element_type=F32
+        )
+        for side, stage in ((0, left_stage), (1, right_stage)):
+            parts = []
+            for block in range(blocks):
+                at = side * 2 * hidden + block * devices
+                value = projected[at : at + devices]
+                gate = projected[at + hidden : at + hidden + devices]
+                parts.append(live[:devices] * jax.nn.sigmoid(gate) * value)
+            swapped = swap_blocks(parts, tile_rows)
+            for inner in range(blocks):
+                k = quarter * blocks + inner
+                stage[pl.ds(k, devices, stride=tile_cols), :] = swapped[inner]
+    send[:, 0] = left_stage[...].reshape(devices, tile_cols, LANES).astype(BF16)
+    send[:, 1] = right_stage[...].reshape(devices, tile_cols, LANES).astype(BF16)
+
+    pl.semaphore_wait(barrier, devices - 1)
+
+    def outgoing(target):
+        return pltpu.make_async_remote_copy(
+            src_ref=send.at[target],
+            dst_ref=recv.at[me],
+            send_sem=send_sem.at[target],
+            recv_sem=recv_sem.at[me],
+            device_id=place(target),
+            device_id_type=MESH,
+        )
+
+    def incoming(source):
+        return pltpu.make_async_remote_copy(
+            src_ref=send.at[source],
+            dst_ref=recv.at[source],
+            send_sem=send_sem.at[source],
+            recv_sem=recv_sem.at[source],
+            device_id=place(source),
+            device_id_type=MESH,
+        )
+
+    def start_first(step, carry):
+        outgoing(lax.rem(me + step, devices)).start()
+        return carry
+
+    lax.fori_loop(1, devices, start_first, 0)
+    recv[me] = send[me]
+    gates = jnp.dot(normed, output_gate[...], preferred_element_type=F32)
+    gate_buf[...] = jax.nn.sigmoid(gates).reshape(tile_rows, tile_cols, channels)
+
+    def wait_first(step, carry):
+        incoming(lax.rem(me + devices - step, devices)).wait_recv()
+        return carry
+
+    lax.fori_loop(1, devices, wait_first, 0)
+
+    def gathered(side, row):
+        return recv[row * plane : (row + 1) * plane, side].reshape(plane * tile_cols, LANES)
+
+    rights = [gathered(1, row) for row in range(row_count)]
+    rights = jnp.concatenate(rights, axis=1)
+    half_bit = (lax.broadcasted_iota(jnp.int32, (tile_cols, LANES), 1) // tile_cols) & 1
+    for row in range(row_count):
+        lefts = jnp.transpose(gathered(0, row).astype(F32)).astype(BF16)
+        products = jnp.dot(lefts, rights, preferred_element_type=F32)
+        for other in range(row_count):
+            piece = products[:, other * LANES : (other + 1) * LANES]
+            mixed = piece[:tile_rows]
+            for block in range(1, blocks):
+                mixed = jnp.where(
+                    lane_block == block, piece[block * tile_rows : (block + 1) * tile_rows], mixed
+                )
+            upper, lower = mixed[:tile_cols], mixed[tile_cols:]
+            first = jnp.where(half_bit == 0, upper, pltpu.roll(lower, tile_cols, 1))
+            second = jnp.where(half_bit == 1, lower, pltpu.roll(upper, LANES - tile_cols, 1))
+            target = row * plane + other * 2
+            back[target] = first.astype(BACK)
+            back[target + 1] = second.astype(BACK)
+
+    def returning(target):
+        return pltpu.make_async_remote_copy(
+            src_ref=back.at[target],
+            dst_ref=home.at[me],
+            send_sem=back_sem.at[target],
+            recv_sem=home_sem.at[me],
+            device_id=place(target),
+            device_id_type=MESH,
+        )
+
+    def coming_home(source):
+        return pltpu.make_async_remote_copy(
+            src_ref=back.at[source],
+            dst_ref=home.at[source],
+            send_sem=back_sem.at[source],
+            recv_sem=home_sem.at[source],
+            device_id=place(source),
+            device_id_type=MESH,
+        )
+
+    def start_second(step, carry):
+        returning(lax.rem(me + step, devices)).start()
+        return carry
+
+    lax.fori_loop(1, devices, start_second, 0)
+    home[me] = back[me]
+
+    def wait_second(step, carry):
+        coming_home(lax.rem(me + devices - step, devices)).wait_recv()
+        return carry
+
+    lax.fori_loop(1, devices, wait_second, 0)
+
+    left_stage[...] = home[...].astype(F32).reshape(devices * tile_cols, LANES)
+    for group in range(tile_cols // blocks):
+        rows = [
+            left_stage[pl.ds(group * blocks + inner, devices, stride=tile_cols), :]
+            for inner in range(blocks)
+        ]
+        turned = jnp.transpose(jnp.concatenate(rows, axis=0))
+        parts = [turned[b * tile_rows : (b + 1) * tile_rows] for b in range(blocks)]
+        together = jnp.concatenate(swap_blocks(parts, devices), axis=0)
+        normed_out = norm_rows(together, final_gain[...], final_shift[...]).astype(BF16)
+        projected_out = jnp.dot(normed_out, output_weight[...], preferred_element_type=F32)
+        for inner in range(blocks):
+            for half in range(2):
+                i = half * tile_cols + group * blocks + inner
+                at = inner * tile_rows + half * tile_cols
+                out_ref[i] = (gate_buf[i] * projected_out[at : at + tile_cols]).astype(BF16)
+
+    def drain(step, carry):
+        target = lax.rem(me + step, devices)
+        outgoing(target).wait_send()
+        returning(target).wait_send()
+        return carry
+
+    lax.fori_loop(1, devices, drain, 0)
+
+
+def fused(sizes, *arrays):
+    row_count, col_count, split_count, tile_rows, tile_cols, channels, hidden = sizes
+    devices = row_count * col_count * split_count
+    state, mask, gain_in, shift_in, weights, gate, gain_out, shift_out, weight_out = arrays
+    vmem = pl.BlockSpec(memory_space=pltpu.VMEM)
+    smem = pl.BlockSpec(memory_space=pltpu.SMEM)
+    return pl.pallas_call(
+        functools.partial(kernel, sizes),
+        out_shape=jax.ShapeDtypeStruct(state.shape, BF16),
+        in_specs=[vmem, smem] + [vmem] * 8,
+        out_specs=vmem,
+        scratch_shapes=[
+            pltpu.VMEM((tile_rows * tile_cols, channels), F32),
+            pltpu.VMEM((tile_rows, tile_cols, channels), F32),
+            pltpu.VMEM((devices * tile_cols, LANES), F32),
+            pltpu.VMEM((devices * tile_cols, LANES), F32),
+            pltpu.VMEM((devices, 2, tile_cols, LANES), BF16),
+            pltpu.VMEM((devices, 2, tile_cols, LANES), BF16),
+            pltpu.VMEM((devices, tile_cols, LANES), BACK),
+            pltpu.VMEM((devices, tile_cols, LANES), BACK),
+            pltpu.SemaphoreType.DMA((devices,)),
+            pltpu.SemaphoreType.DMA((devices,)),
+            pltpu.SemaphoreType.DMA((devices,)),
+            pltpu.SemaphoreType.DMA((devices,)),
+        ],
+        compiler_params=pltpu.CompilerParams(collective_id=0, has_side_effects=True),
+    )(
+        state,
+        mask,
+        mask[None],
+        gain_in[None],
+        shift_in[None],
+        weights,
+        gate,
+        gain_out[None],
+        shift_out[None],
+        weight_out,
+    )
+
+
+def update(*arrays):
+    state, mask, weight_out = arrays[0], arrays[1], arrays[8]
+    tile_rows, tile_cols, channels = state.shape
+    hidden = weight_out.shape[0]
+    row_count, col_count = lax.axis_size("row"), lax.axis_size("col")
+    split_count = lax.axis_size("ksplit")
+    devices = row_count * col_count * split_count
+    fits = (
+        channels == LANES
+        and hidden == LANES
+        and mask.shape[0] == LANES
+        and row_count * tile_rows == LANES
+        and devices == tile_rows
+        and tile_rows == 2 * tile_cols
+        and tile_cols % 16 == 0
+    )
+    if fits:
+        sizes = (row_count, col_count, split_count, tile_rows, tile_cols, channels, hidden)
+        return fused(sizes, *arrays)
+    return body(*arrays)
 
 
 def norm_over(data, norm_gain, norm_shift, over_axis):
@@ -110,7 +419,7 @@
         P(),
     )
     return jax.shard_map(
-        body,
+        update,
         mesh=mesh,
         in_specs=placed,
         out_specs=P(("groups", "row"), ("col", "ksplit"), None),

time: 54.1 us -> 26.4 us (0.49)
  Pallas kernels: 0 us -> 24.7 us
  waiting for transfers between devices: 23.4 us -> 0 us
  starting transfers between devices: 12.5 us -> 0 us
  local copies, waits for them, and re-layouts: 10.1 us -> 1.57 us
  other arithmetic: 4.81 us -> 0 us
  matrix products: 2.71 us -> 0 us
    pallas_call x0 -> x1, Pallas kernels: none -> 24.7 us  [fused(): pl.pallas_call(functools.partial(kernel, sizes), out_shape=jax.ShapeDtype...]
    all_to_all x3 -> x0, waiting for transfers between devices: 23.4 us -> none  [the longest x1 10.2 us: body(): lax.all_to_all(returned, ('row', 'col', 'ksplit'), split_axis=0, concat_a...]
    all_to_all x3 -> x0, starting transfers between devices: 12.5 us -> none  [the longest x1 7.33 us: body(): lax.all_to_all(grouped_left, ('row', 'col', 'ksplit'), split_axis=0, conc...]
    unnamed x22 -> x1, local copies, waits for them, and re-layouts: 5.88 us -> 1.57 us
    dot_general x7 -> x0, matrix products: 2.71 us -> none  [the longest x1 0.83 us: body(): jnp.einsum('hij,hc->ijc', normed_out, output_weight, preferred_element_ty...]
    convert_element_type x3 -> x0, other arithmetic: 1.83 us -> none  [the longest x1 0.76 us: body(): lax.dynamic_slice_in_dim(residue_mask, col_start, tile_cols)]
    reshape x5 -> x0, local copies, waits for them, and re-layouts: 1.82 us -> none  [the longest x2 0.56 us: assemble(): parts.transpose(2, 0, 3, 1, 4)]
    reduce_sum x4 -> x0, other arithmetic: 1.62 us -> none  [the longest x2 1.18 us: norm_over(): average = jnp.mean(data, axis=over_axis, keepdims=True)]
  transfers between devices with their start and end apart: 3 -> 0, of which waited for: 3 -> 0; matrix products, arithmetic and copies ran while one was open for 7% -> 0% of each run, Pallas kernels for 0% -> 0%
where the time goes in v1:
time: 26.4 us; the launch traced here: 26.3 us
  Pallas kernels  24.7 us (94%)
  local copies, waits for them, and re-layouts  1.57 us (6%)
    pallas_call x1, Pallas kernels, fused(): pl.pallas_call(functools.partial(kernel, sizes), out_shape=jax.ShapeDtype...  24.7 us
    unnamed x1, local copies, waits for them, and re-layouts  1.57 us

profile of v1, /device:TPU:0, one launch (start us, length us, event | category | flops | bytes accessed | tf_op | source)
XLA Modules:
  0.0 26.3 jit_solution(6189915499427567402)
XLA Ops:
  0.0 24.7 %shard_map.91 = bf16[32,16,128]{2,1,0:T(8,128)(2,1)} custom-call(bf16[32,16,128]{2,1,0:T(8,128)(2,1)} %state_ref.1, s32[128]{0:T(128)} %mask_scalars.1, s32[1,128]{1,0:T(1,128)} %bitcast.5, f32[1,128]{1,0:T(1,128)} %bitcast.6, f32[1,128]{1,0:T(1,128)} %bitcast.7, bf16[128,512]{1,0:T(8,128)(2,1)} %left_right.1, bf16[128,128]{1,0:T(8,128)(2,1)} %output_gate.1, ...), custom_call_target="tpu_custom_call" | custom-call | tf_op jit(solution)/shard_map/pallas_call | solution.py:260
  24.7 1.6 %copy.11 = bf16[32,16,128]{2,1,0:T(8,128)(2,1)} copy(bf16[32,16,128]{2,1,0:T(8,128)(2,1)} %shard_map.91) | data formatting | bytes 262144

commit v2 on v0

--- a/solution.py
+++ b/solution.py
@@ -1,7 +1,333 @@
+import functools
+
 import jax
 import jax.numpy as jnp
 from jax import lax
+from jax.experimental import pallas as pl
+from jax.experimental.pallas import tpu as pltpu
 from jax.sharding import PartitionSpec as P
+
+MESH = pl.DeviceIdType.MESH
+LANES = 128
+F32 = jnp.float32
+BF16 = jnp.bfloat16
+BACK = jnp.bfloat16
+
+
+def norm_rows(data, gain, shift):
+    average = jnp.mean(data, axis=-1, keepdims=True)
+    centred = data - average
+    spread = jnp.mean(centred * centred, axis=-1, keepdims=True)
+    return centred * lax.rsqrt(spread + 1e-05) * gain + shift
+
+
+def swap_blocks(parts, width):
+    count = len(parts)
+    lane_block = lax.broadcasted_iota(jnp.int32, parts[0].shape, 1) // width
+    parts = list(parts)
+    step = count // 2
+    while step:
+        upper = (lane_block & step) != 0
+        for low in range(count):
+            if low & step:
+                continue
+            first, second = parts[low], parts[low + step]
+            parts[low] = jnp.where(upper, pltpu.roll(second, step * width, 1), first)
+            parts[low + step] = jnp.where(
+                upper, second, pltpu.roll(first, LANES - step * width, 1)
+            )
+        step //= 2
+    return parts
+
+
+def kernel(sizes, *refs):
+    row_count, col_count, split_count, tile_rows, tile_cols, channels, hidden = sizes
+    hbm_inputs, out_ref, inputs = refs[:9], refs[9], refs[10:19]
+    normed_buf, gate_buf, left_stage, right_stage = refs[19:23]
+    left_send, right_send, left_recv, right_recv, back, home = refs[23:29]
+    load_sem, left_out, left_in, right_out, right_in, back_out, back_in = refs[29:36]
+    state_ref, mask_ref, input_gain, input_shift, left_right = inputs[:5]
+    output_gate, final_gain, final_shift, output_weight = inputs[5:]
+    plane = col_count * split_count
+    devices = row_count * plane
+    owners = devices // 2
+    half_rows = row_count // 2
+    blocks = LANES // tile_rows
+    my_row = lax.axis_index("row")
+    my_plane = lax.axis_index("col") * split_count + lax.axis_index("ksplit")
+    me = my_row * plane + my_plane
+    my_base = (my_row // half_rows) * owners
+    my_group = lax.rem(me, owners)
+    my_inner = lax.rem(my_row, half_rows)
+
+    def place(index):
+        within = lax.rem(index, plane)
+        return {
+            "row": index // plane,
+            "col": within // split_count,
+            "ksplit": lax.rem(within, split_count),
+        }
+
+    loads = [
+        pltpu.make_async_copy(source, target, load_sem.at[at])
+        for at, (source, target) in enumerate(zip(hbm_inputs, inputs))
+    ]
+    for load in loads:
+        load.start()
+
+    barrier = pltpu.get_barrier_semaphore()
+
+    def greet(step, carry):
+        pl.semaphore_signal(
+            barrier, inc=1, device_id=place(lax.rem(me + step, devices)), device_id_type=MESH
+        )
+        return carry
+
+    lax.fori_loop(1, devices, greet, 0)
+    for load in loads:
+        load.wait()
+
+    positions = tile_rows * tile_cols
+    state = state_ref[...].astype(F32).reshape(positions, channels)
+    normed = norm_rows(state, input_gain[...], input_shift[...]).astype(BF16)
+    normed_buf[...] = normed.astype(F32)
+    weights = jnp.transpose(left_right[...].astype(F32)).astype(BF16)
+
+    lane = lax.broadcasted_iota(jnp.int32, (1, LANES), 1)
+    lane_block = lax.broadcasted_iota(jnp.int32, (tile_rows, LANES), 1) // tile_rows
+    mask_line = mask_ref[...].astype(F32)
+    mask_rows = jnp.broadcast_to(mask_line, (tile_rows, LANES))
+    row_live = mask_rows
+    turn = lax.rem(lane_block - my_row + row_count, row_count)
+    for shift in range(1, blocks):
+        row_live = jnp.where(turn == shift, pltpu.roll(mask_rows, shift * tile_rows, 1), row_live)
+
+    for quarter in range(tile_cols // blocks):
+        rows = []
+        col_live = jnp.zeros((tile_rows, LANES), F32)
+        for inner in range(blocks):
+            k = quarter * blocks + inner
+            rows.append(normed_buf[pl.ds(k, tile_rows, stride=tile_cols), :])
+            alive = jnp.where(lane == my_plane * tile_cols + k, mask_line, 0.0)
+            alive = jnp.sum(alive, axis=1, keepdims=True)
+            col_live = jnp.where(lane_block == inner, alive, col_live)
+        live = row_live * col_live
+        packed = jnp.concatenate(rows, axis=0).astype(BF16)
+        projected = lax.dot_general(
+            weights, packed, (((1,), (1,)), ((), ())), preferred_element_type=F32
+        )
+        for side, stage in ((0, left_stage), (1, right_stage)):
+            parts = []
+            for block in range(blocks):
+                at = side * 2 * hidden + block * tile_rows
+                value = projected[at : at + tile_rows]
+                gate = projected[at + hidden : at + hidden + tile_rows]
+                parts.append(live * jax.nn.sigmoid(gate) * value)
+            swapped = swap_blocks(parts, tile_rows)
+            for inner in range(blocks):
+                k = quarter * blocks + inner
+                stage[pl.ds(k, tile_rows, stride=tile_cols), :] = swapped[inner]
+    right_send[...] = right_stage[...].reshape(right_send.shape).astype(BF16)
+    left_send[...] = left_stage[...].reshape(left_send.shape).astype(BF16)
+
+    pl.semaphore_wait(barrier, devices - 1)
+
+    def right_copy(target, source, arriving):
+        row = source // plane
+        return pltpu.make_async_remote_copy(
+            src_ref=right_send.at[:, lax.rem(target, owners)],
+            dst_ref=right_recv.at[:, row, lax.rem(source, plane)],
+            send_sem=right_out.at[target],
+            recv_sem=right_in.at[source],
+            device_id=place(source if arriving else target),
+            device_id_type=MESH,
+        )
+
+    def left_copy(target, source, arriving):
+        row = lax.rem(source, owners) // plane
+        return pltpu.make_async_remote_copy(
+            src_ref=left_send.at[:, target],
+            dst_ref=left_recv.at[:, row, lax.rem(source, plane)],
+            send_sem=left_out.at[target],
+            recv_sem=left_in.at[lax.rem(source, owners)],
+            device_id=place(my_base + (lax.rem(source, owners) if arriving else target)),
+            device_id_type=MESH,
+        )
+
+    def back_copy(target, source, arriving):
+        return pltpu.make_async_remote_copy(
+            src_ref=back.at[target],
+            dst_ref=home.at[source],
+            send_sem=back_out.at[target],
+            recv_sem=back_in.at[source],
+            device_id=place(my_base + (source if arriving else target)),
+            device_id_type=MESH,
+        )
+
+    far_base = owners - my_base
+
+    def send_far(step, carry):
+        right_copy(far_base + lax.rem(my_group + step, owners), me, False).start()
+        return carry
+
+    def send_near(step, carry):
+        target = lax.rem(my_group + step, owners)
+        right_copy(my_base + target, me, False).start()
+        left_copy(target, me, False).start()
+        return carry
+
+    lax.fori_loop(0, owners, send_far, 0)
+    lax.fori_loop(1, owners, send_near, 0)
+    right_recv[:, my_row, my_plane] = right_send[:, my_group]
+    left_recv[:, my_inner, my_plane] = left_send[:, my_group]
+    gates = jnp.dot(normed, output_gate[...], preferred_element_type=F32)
+    gate_buf[...] = jax.nn.sigmoid(gates)
+
+    def wait_near(step, carry):
+        source = lax.rem(my_group + owners - step, owners)
+        left_copy(source, source, True).wait_recv()
+        right_copy(my_base + source, my_base + source, True).wait_recv()
+        return carry
+
+    def wait_far(step, carry):
+        source = far_base + lax.rem(my_group + owners - step, owners)
+        right_copy(source, source, True).wait_recv()
+        return carry
+
+    lax.fori_loop(1, owners, wait_near, 0)
+    lax.fori_loop(0, owners, wait_far, 0)
+
+    depth = plane * tile_cols
+    rights = [
+        jnp.concatenate(
+            [right_recv[bit, row].reshape(depth, LANES) for row in range(row_count)], axis=1
+        )
+        for bit in range(2)
+    ]
+    half_bit = (lax.broadcasted_iota(jnp.int32, (tile_rows, LANES), 1) // tile_cols) & 1
+    for inner in range(half_rows):
+        products = []
+        for bit in range(2):
+            lefts = left_recv[bit, inner].reshape(depth, LANES)
+            lefts = jnp.transpose(lefts.astype(F32)).astype(BF16)
+            products.append(jnp.dot(lefts, rights[bit], preferred_element_type=F32))
+        for other in range(row_count):
+            mixed = []
+            for product in products:
+                piece = product[:, other * LANES : (other + 1) * LANES]
+                chosen = piece[:tile_rows]
+                for block in range(1, blocks):
+                    chosen = jnp.where(
+                        lane_block == block,
+                        piece[block * tile_rows : (block + 1) * tile_rows],
+                        chosen,
+                    )
+                mixed.append(chosen)
+            first = jnp.where(half_bit == 0, mixed[0], pltpu.roll(mixed[1], tile_cols, 1))
+            second = jnp.where(
+                half_bit == 1, mixed[1], pltpu.roll(mixed[0], LANES - tile_cols, 1)
+            )
+            target = inner * plane + other * 2
+            back[target] = first.astype(BACK)
+            back[target + 1] = second.astype(BACK)
+
+    def send_back(step, carry):
+        back_copy(lax.rem(my_group + step, owners), my_group, False).start()
+        return carry
+
+    def wait_back(step, carry):
+        source = lax.rem(my_group + owners - step, owners)
+        back_copy(source, source, True).wait_recv()
+        return carry
+
+    lax.fori_loop(1, owners, send_back, 0)
+    home[my_group] = back[my_group]
+    lax.fori_loop(1, owners, wait_back, 0)
+
+    left_stage[...] = home[...].astype(F32).reshape(owners * tile_rows, LANES)
+    step_rows = LANES // tile_cols
+    for group in range(tile_rows // step_rows):
+        rows = [
+            left_stage[pl.ds(group * step_rows + at, owners, stride=tile_rows), :]
+            for at in range(step_rows)
+        ]
+        turned = jnp.transpose(jnp.concatenate(rows, axis=0))
+        parts = [turned[b * tile_cols : (b + 1) * tile_cols] for b in range(step_rows)]
+        together = jnp.concatenate(swap_blocks(parts, owners), axis=0)
+        normed_out = norm_rows(together, final_gain[...], final_shift[...]).astype(BF16)
+        projected_out = jnp.dot(normed_out, output_weight[...], preferred_element_type=F32)
+        gated = gate_buf[group * LANES : (group + 1) * LANES] * projected_out
+        out_ref[group * step_rows : (group + 1) * step_rows] = gated.reshape(
+            step_rows, tile_cols, channels
+        ).astype(BF16)
+
+    def drain_near(step, carry):
+        target = lax.rem(my_group + step, owners)
+        right_copy(my_base + target, me, False).wait_send()
+        left_copy(target, me, False).wait_send()
+        back_copy(target, my_group, False).wait_send()
+        return carry
+
+    def drain_far(step, carry):
+        right_copy(far_base + lax.rem(my_group + step, owners), me, False).wait_send()
+        return carry
+
+    lax.fori_loop(1, owners, drain_near, 0)
+    lax.fori_loop(0, owners, drain_far, 0)
+
+
+def fused(sizes, *arrays):
+    row_count, col_count, split_count, tile_rows, tile_cols, channels, hidden = sizes
+    plane = col_count * split_count
+    devices = row_count * plane
+    owners = devices // 2
+    state, *lines, weights, gate, gain_out, shift_out, weight_out = arrays
+    lines = [line[None] for line in lines]
+    operands = [state, *lines, weights, gate, gain_out[None], shift_out[None], weight_out]
+    flat = (tile_rows * tile_cols, LANES)
+    tile = (tile_cols, LANES)
+    counts = (len(operands), owners, owners, devices, devices, owners, owners)
+    return pl.pallas_call(
+        functools.partial(kernel, sizes),
+        out_shape=jax.ShapeDtypeStruct(state.shape, BF16),
+        in_specs=[pl.BlockSpec(memory_space=pl.ANY)] * len(operands),
+        out_specs=pl.BlockSpec(memory_space=pltpu.VMEM),
+        scratch_shapes=[pltpu.VMEM(item.shape, item.dtype) for item in operands]
+        + [pltpu.VMEM(flat, F32)] * 4
+        + [pltpu.VMEM((2, owners) + tile, BF16)] * 2
+        + [
+            pltpu.VMEM((2, row_count // 2, plane) + tile, BF16),
+            pltpu.VMEM((2, row_count, plane) + tile, BF16),
+            pltpu.VMEM((owners, tile_rows, LANES), BACK),
+            pltpu.VMEM((owners, tile_rows, LANES), BACK),
+        ]
+        + [pltpu.SemaphoreType.DMA((count,)) for count in counts],
+        compiler_params=pltpu.CompilerParams(collective_id=0, has_side_effects=True),
+    )(*operands)
+
+
+def update(*arrays):
+    state, mask, weight_out = arrays[0], arrays[1], arrays[8]
+    tile_rows, tile_cols, channels = state.shape
+    hidden = weight_out.shape[0]
+    row_count, col_count = lax.axis_size("row"), lax.axis_size("col")
+    split_count = lax.axis_size("ksplit")
+    devices = row_count * col_count * split_count
+    fits = (
+        channels == LANES
+        and hidden == LANES
+        and mask.shape[0] == LANES
+        and row_count * tile_rows == LANES
+        and devices == tile_rows
+        and row_count % 2 == 0
+        and devices // 2 == tile_cols
+        and tile_rows == 2 * tile_cols
+        and tile_cols % 16 == 0
+    )
+    if fits:
+        sizes = (row_count, col_count, split_count, tile_rows, tile_cols, channels, hidden)
+        return fused(sizes, *arrays)
+    return body(*arrays)
 
 
 def norm_over(data, norm_gain, norm_shift, over_axis):
@@ -110,7 +436,7 @@
         P(),
     )
     return jax.shard_map(
-        body,
+        update,
         mesh=mesh,
         in_specs=placed,
         out_specs=P(("groups", "row"), ("col", "ksplit"), None),

time: 54.1 us -> 24.5 us (0.45)
  waiting for transfers between devices: 23.4 us -> 0 us
  Pallas kernels: 0 us -> 22.8 us
  starting transfers between devices: 12.5 us -> 0 us
  local copies, waits for them, and re-layouts: 10.1 us -> 1.57 us
  other arithmetic: 4.81 us -> 0 us
  matrix products: 2.71 us -> 0 us
    all_to_all x3 -> x0, waiting for transfers between devices: 23.4 us -> none  [the longest x1 10.2 us: body(): lax.all_to_all(returned, ('row', 'col', 'ksplit'), split_axis=0, concat_a...]
    pallas_call x0 -> x1, Pallas kernels: none -> 22.8 us  [fused(): pl.pallas_call(functools.partial(kernel, sizes), out_shape=jax.ShapeDtype...]
    all_to_all x3 -> x0, starting transfers between devices: 12.5 us -> none  [the longest x1 7.33 us: body(): lax.all_to_all(grouped_left, ('row', 'col', 'ksplit'), split_axis=0, conc...]
    unnamed x22 -> x1, local copies, waits for them, and re-layouts: 5.88 us -> 1.57 us
    dot_general x7 -> x0, matrix products: 2.71 us -> none  [the longest x1 0.83 us: body(): jnp.einsum('hij,hc->ijc', normed_out, output_weight, preferred_element_ty...]
    convert_element_type x3 -> x0, other arithmetic: 1.83 us -> none  [the longest x1 0.76 us: body(): lax.dynamic_slice_in_dim(residue_mask, col_start, tile_cols)]
    reshape x5 -> x0, local copies, waits for them, and re-layouts: 1.82 us -> none  [the longest x2 0.56 us: assemble(): parts.transpose(2, 0, 3, 1, 4)]
    reduce_sum x4 -> x0, other arithmetic: 1.62 us -> none  [the longest x2 1.18 us: norm_over(): average = jnp.mean(data, axis=over_axis, keepdims=True)]
  transfers between devices with their start and end apart: 3 -> 0, of which waited for: 3 -> 0; matrix products, arithmetic and copies ran while one was open for 7% -> 0% of each run, Pallas kernels for 0% -> 0%
where the time goes in v2:
time: 24.5 us; the launch traced here: 24.3 us
  Pallas kernels  22.8 us (93%)
  local copies, waits for them, and re-layouts  1.57 us (6%)
    pallas_call x1, Pallas kernels, fused(): pl.pallas_call(functools.partial(kernel, sizes), out_shape=jax.ShapeDtype...  22.8 us
    unnamed x1, local copies, waits for them, and re-layouts  1.57 us

profile of v2, /device:TPU:0, one launch (start us, length us, event | category | flops | bytes accessed | tf_op | source)
XLA Modules:
  0.0 24.3 jit_solution(15226655812219987658)
XLA Ops:
  0.0 22.8 %shard_map.91 = bf16[32,16,128]{2,1,0:T(8,128)(2,1)} custom-call(bf16[32,16,128]{2,1,0:T(8,128)(2,1)} %refs_0_.1, s32[1,128]{1,0:T(1,128)} %bitcast.5, f32[1,128]{1,0:T(1,128)} %bitcast.6, f32[1,128]{1,0:T(1,128)} %bitcast.7, bf16[128,512]{1,0:T(8,128)(2,1)} %refs_4_.1, bf16[128,128]{1,0:T(8,128)(2,1)} %refs_5_.1, f32[1,128]{1,0:T(1,128)} %bitcast.8, ...), custom_call_target="tpu_custom_call" | custom-call | tf_op jit(solution)/shard_map/pallas_call | solution.py:290
  22.8 1.6 %copy.11 = bf16[32,16,128]{2,1,0:T(8,128)(2,1)} copy(bf16[32,16,128]{2,1,0:T(8,128)(2,1)} %shard_map.91) | data formatting | bytes 262144

commit v3 on v2

--- a/solution.py
+++ b/solution.py
@@ -102,6 +102,7 @@
     for shift in range(1, blocks):
         row_live = jnp.where(turn == shift, pltpu.roll(mask_rows, shift * tile_rows, 1), row_live)
 
+    lives, packs = [], []
     for quarter in range(tile_cols // blocks):
         rows = []
         col_live = jnp.zeros((tile_rows, LANES), F32)
@@ -111,25 +112,28 @@
             alive = jnp.where(lane == my_plane * tile_cols + k, mask_line, 0.0)
             alive = jnp.sum(alive, axis=1, keepdims=True)
             col_live = jnp.where(lane_block == inner, alive, col_live)
-        live = row_live * col_live
-        packed = jnp.concatenate(rows, axis=0).astype(BF16)
-        projected = lax.dot_general(
-            weights, packed, (((1,), (1,)), ((), ())), preferred_element_type=F32
-        )
-        for side, stage in ((0, left_stage), (1, right_stage)):
+        lives.append(row_live * col_live)
+        packs.append(jnp.concatenate(rows, axis=0).astype(BF16))
+
+    def make_side(side, stage, ready):
+        own = weights[side * 2 * hidden : (side + 1) * 2 * hidden]
+        for quarter in range(tile_cols // blocks):
+            projected = lax.dot_general(
+                own, packs[quarter], (((1,), (1,)), ((), ())), preferred_element_type=F32
+            )
             parts = []
             for block in range(blocks):
-                at = side * 2 * hidden + block * tile_rows
+                at = block * tile_rows
                 value = projected[at : at + tile_rows]
                 gate = projected[at + hidden : at + hidden + tile_rows]
-                parts.append(live * jax.nn.sigmoid(gate) * value)
+                parts.append(lives[quarter] * jax.nn.sigmoid(gate) * value)
             swapped = swap_blocks(parts, tile_rows)
             for inner in range(blocks):
                 k = quarter * blocks + inner
                 stage[pl.ds(k, tile_rows, stride=tile_cols), :] = swapped[inner]
-    right_send[...] = right_stage[...].reshape(right_send.shape).astype(BF16)
-    left_send[...] = left_stage[...].reshape(left_send.shape).astype(BF16)
-
+        ready[...] = stage[...].reshape(ready.shape).astype(BF16)
+
+    make_side(1, right_stage, right_send)
     pl.semaphore_wait(barrier, devices - 1)
 
     def right_copy(target, source, arriving):
@@ -171,50 +175,61 @@
         return carry
 
     def send_near(step, carry):
-        target = lax.rem(my_group + step, owners)
-        right_copy(my_base + target, me, False).start()
-        left_copy(target, me, False).start()
+        right_copy(my_base + lax.rem(my_group + step, owners), me, False).start()
+        return carry
+
+    def send_left(step, carry):
+        left_copy(lax.rem(my_group + step, owners), me, False).start()
         return carry
 
     lax.fori_loop(0, owners, send_far, 0)
     lax.fori_loop(1, owners, send_near, 0)
     right_recv[:, my_row, my_plane] = right_send[:, my_group]
+    make_side(0, left_stage, left_send)
+    lax.fori_loop(1, owners, send_left, 0)
     left_recv[:, my_inner, my_plane] = left_send[:, my_group]
     gates = jnp.dot(normed, output_gate[...], preferred_element_type=F32)
     gate_buf[...] = jax.nn.sigmoid(gates)
 
-    def wait_near(step, carry):
+    def wait_left(step, carry):
         source = lax.rem(my_group + owners - step, owners)
         left_copy(source, source, True).wait_recv()
-        right_copy(my_base + source, my_base + source, True).wait_recv()
-        return carry
-
-    def wait_far(step, carry):
-        source = far_base + lax.rem(my_group + owners - step, owners)
-        right_copy(source, source, True).wait_recv()
-        return carry
-
-    lax.fori_loop(1, owners, wait_near, 0)
-    lax.fori_loop(0, owners, wait_far, 0)
+        return carry
+
+    lax.fori_loop(1, owners, wait_left, 0)
 
     depth = plane * tile_cols
-    rights = [
-        jnp.concatenate(
-            [right_recv[bit, row].reshape(depth, LANES) for row in range(row_count)], axis=1
-        )
-        for bit in range(2)
-    ]
     half_bit = (lax.broadcasted_iota(jnp.int32, (tile_rows, LANES), 1) // tile_cols) & 1
-    for inner in range(half_rows):
-        products = []
-        for bit in range(2):
-            lefts = left_recv[bit, inner].reshape(depth, LANES)
-            lefts = jnp.transpose(lefts.astype(F32)).astype(BF16)
-            products.append(jnp.dot(lefts, rights[bit], preferred_element_type=F32))
-        for other in range(row_count):
+    lefts = []
+    for bit in range(2):
+        both = [
+            jnp.transpose(left_recv[bit, inner].reshape(depth, LANES).astype(F32))
+            for inner in range(half_rows)
+        ]
+        lefts.append(jnp.concatenate(both, axis=0).astype(BF16))
+
+    for turn in range(row_count):
+        if turn < half_rows:
+            row = my_base // plane + lax.rem(my_inner + turn, half_rows)
+        else:
+            row = far_base // plane + lax.rem(my_inner + turn, half_rows)
+
+        def wait_right(step, carry):
+            source = row * plane + lax.rem(my_plane + step, plane)
+            right_copy(source, source, True).wait_recv()
+            return carry
+
+        lax.fori_loop(1 if turn == 0 else 0, plane, wait_right, 0)
+        products = [
+            jnp.dot(
+                lefts[bit], right_recv[bit, row].reshape(depth, LANES), preferred_element_type=F32
+            )
+            for bit in range(2)
+        ]
+        for inner in range(half_rows):
             mixed = []
             for product in products:
-                piece = product[:, other * LANES : (other + 1) * LANES]
+                piece = product[inner * LANES : (inner + 1) * LANES]
                 chosen = piece[:tile_rows]
                 for block in range(1, blocks):
                     chosen = jnp.where(
@@ -227,21 +242,23 @@
             second = jnp.where(
                 half_bit == 1, mixed[1], pltpu.roll(mixed[0], LANES - tile_cols, 1)
             )
-            target = inner * plane + other * 2
-            back[target] = first.astype(BACK)
-            back[target + 1] = second.astype(BACK)
-
-    def send_back(step, carry):
-        back_copy(lax.rem(my_group + step, owners), my_group, False).start()
-        return carry
+            for half, part in ((0, first), (1, second)):
+                target = inner * plane + row * 2 + half
+                back[target] = part.astype(BACK)
+
+                @pl.when(target != my_group)
+                def _():
+                    back_copy(target, my_group, False).start()
+
+                @pl.when(target == my_group)
+                def _():
+                    home[my_group] = back[my_group]
 
     def wait_back(step, carry):
         source = lax.rem(my_group + owners - step, owners)
         back_copy(source, source, True).wait_recv()
         return carry
 
-    lax.fori_loop(1, owners, send_back, 0)
-    home[my_group] = back[my_group]
     lax.fori_loop(1, owners, wait_back, 0)
 
     left_stage[...] = home[...].astype(F32).reshape(owners * tile_rows, LANES)
@@ -289,7 +306,7 @@
     counts = (len(operands), owners, owners, devices, devices, owners, owners)
     return pl.pallas_call(
         functools.partial(kernel, sizes),
-        out_shape=jax.ShapeDtypeStruct(state.shape, BF16),
+        out_shape=pltpu.VMEM(state.shape, BF16),
         in_specs=[pl.BlockSpec(memory_space=pl.ANY)] * len(operands),
         out_specs=pl.BlockSpec(memory_space=pltpu.VMEM),
         scratch_shapes=[pltpu.VMEM(item.shape, item.dtype) for item in operands]

time: 24.5 us -> 23 us (0.939)
  local copies, waits for them, and re-layouts: 1.57 us -> 0.66 us
  Pallas kernels: 22.8 us -> 22.2 us
    unnamed x1, local copies, waits for them, and re-layouts: 1.57 us -> 0.66 us
    pallas_call x1, Pallas kernels: 22.8 us -> 22.2 us  [fused(): pl.pallas_call(functools.partial(kernel, sizes), out_shape=pltpu.VMEM(sta...]
where the time goes in v3:
time: 23 us; the launch traced here: 22.9 us
  Pallas kernels  22.2 us (97%)
  local copies, waits for them, and re-layouts  0.66 us (3%)
    pallas_call x1, Pallas kernels, fused(): pl.pallas_call(functools.partial(kernel, sizes), out_shape=pltpu.VMEM(sta...  22.2 us
    unnamed x1, local copies, waits for them, and re-layouts  0.66 us

profile of v3, /device:TPU:0, one launch (start us, length us, event | category | flops | bytes accessed | tf_op | source)
XLA Modules:
  0.0 22.9 jit_solution(9343367676868543208)
XLA Ops:
  0.0 22.2 %shard_map.91 = bf16[32,16,128]{2,1,0:T(8,128)(2,1)S(1)} custom-call(bf16[32,16,128]{2,1,0:T(8,128)(2,1)} %refs_0_.1, s32[1,128]{1,0:T(1,128)} %bitcast.5, f32[1,128]{1,0:T(1,128)} %bitcast.6, f32[1,128]{1,0:T(1,128)} %bitcast.7, bf16[128,512]{1,0:T(8,128)(2,1)} %refs_4_.1, bf16[128,128]{1,0:T(8,128)(2,1)} %refs_5_.1, f32[1,128]{1,0:T(1,128)} %bitcast.8, ...), custom_call_target="tpu_custom_call" | custom-call | tf_op jit(solution)/shard_map/pallas_call | solution.py:307
  22.2 0.7 %copy.11 = bf16[32,16,128]{2,1,0:T(8,128)(2,1)} copy(bf16[32,16,128]{2,1,0:T(8,128)(2,1)S(1)} %shard_map.91) | data formatting | bytes 262144
